TPU v7x, 32 devices: a whole 2x2x4 slice. The times are simulated.
32 devices in a mesh: trial: 4 (over z), ep: 4 (over y, core), fsdp: 2 (over x).
Axes of the slice: x: 2, y: 2, z: 4, core: 2. Of those that a mesh axis runs over, the one named last changes fastest.
Arguments:
- master_down: float32 [256, 1024, 2048], P(('trial', 'ep'), None, 'fsdp'), parts along dimension 0, may hold values from -0.25 to 0.25
- router_weight: float32 [8192, 64], P(('trial', 'fsdp'), 'ep'), parts along dimension 0, may hold values from -0.125 to 0.125
- router_gain: float32 [8192], P(('trial', 'fsdp')), parts along dimension 0, may hold values from 0.25 to 1.75
Outputs:
- final_down: bfloat16 [256, 1024, 2048], P(('trial', 'ep'), 'fsdp'), parts along dimension 0
- scale_down: float32 [256, 1024], P(('trial', 'ep'), 'fsdp'), parts along dimension 0
- serve_router: bfloat16 [8192, 64], P('trial'), parts along dimension 0
There are 4 independent parts, one for each index of `trial`. A program takes and returns all parts, laid end to end along the dimension named above; each array names one. Nothing has to cross between parts.
All inputs are finite; a program needn't handle non-finite values. Where the computation divides by a largest or mean magnitude, that divisor is 1e-20 or more.
Results may differ from a plain program's by a relative error of at most 0.001.
Values may be sent and summed in bfloat16 or wider, within the bound.
A program may use at most 256 MiB of HBM per device.

v0:
```python
import jax
import jax.numpy as jnp
from jax import lax
from jax.sharding import PartitionSpec as P


def shards(master_down, router_weight, router_gain):
    scale_down = lax.pmax(jnp.max(jnp.abs(master_down), axis=2), "fsdp")
    narrow_down = (master_down / jnp.expand_dims(scale_down, 2)).astype(jnp.bfloat16)
    final_down = lax.all_to_all(narrow_down, "fsdp", split_axis=1, concat_axis=2, tiled=True)
    scale_down = lax.dynamic_slice_in_dim(
        scale_down, lax.axis_index("fsdp") * final_down.shape[1], final_down.shape[1], axis=1
    )
    part_router = (router_weight * router_gain[:, None]).astype(jnp.bfloat16)
    row_router = lax.all_gather(part_router, "fsdp", axis=0, tiled=True)
    serve_router = lax.all_gather(row_router, "ep", axis=1, tiled=True)
    return (final_down, scale_down, serve_router)


def solution(mesh):
    return jax.shard_map(
        shards,
        mesh=mesh,
        in_specs=(
            P(("trial", "ep"), None, "fsdp"),
            P(("trial", "fsdp"), "ep"),
            P(("trial", "fsdp")),
        ),
        out_specs=(P(("trial", "ep"), "fsdp", None), P(("trial", "ep"), "fsdp"), P("trial", None)),
        check_vma=False,
    )
```

profile of v0, /device:TPU:0, one launch (start us, length us, event | category | flops | bytes accessed | tf_op | source)
XLA Modules:
  0.0 617.7 jit_solution(5879946227713915781)
XLA Ops:
  7.2 0.0 all-reduce.2.cloned.1.call-start
  7.2 21.4 %abs_reduce_fusion = f32[16,1024]{1,0:T(8,128)} fusion(f32[16,1024,1024]{2,1,0:T(8,128)} %param.3), kind=kLoop, calls=%fused_computation.2 | loop fusion | flops 33538048 | bytes 67174400 | tf_op jit(solution)/shard_map/reduce_max | solution.py:8
  28.6 0.0 all-reduce.2.cloned.1.call-update
  28.6 23.8 %all-reduce.2.cloned.1.call-done = f32[16,1024]{1,0:T(8,128)} async-done(((f32[16,1024]{1,0:T(8,128)}), f32[16,1024]{1,0:T(8,128)}) %all-reduce.2.cloned.1.call-update) | async-done | bytes 65552 | tf_op jit(solution)/shard_map/pmax | solution.py:8
  52.5 1.0 copy.7
  53.5 0.0 copy-start.1
  53.5 0.0 copy-start.2
  53.5 0.0 copy-start
  53.6 60.1 %fusion = bf16[16,1024,1024]{2,0,1:T(8,128)(2,1)} fusion(f32[16,1024,1024]{2,1,0:T(8,128)} %param.3, f32[16,1024]{0,1:T(8,128)S(1)} %copy.7), kind=kLoop, calls=%fused_computation.1 | loop fusion | flops 33554432 | bytes 100728832 | tf_op jit(solution)/shard_map/convert_element_type | solution.py:9
  113.7 13.0 %all-to-all-start = ((bf16[16,1024,1024]{2,0,1:T(8,128)(2,1)}), bf16[16,1024,1024]{2,0,1:T(8,128)(2,1)}, u32[]{:S(2)}, u32[]{:S(2)}) async-start(bf16[16,1024,1024]{2,0,1:T(8,128)(2,1)} %fusion), calls=%async_computation | async-start | bytes 67108864 | tf_op jit(solution)/shard_map/all_to_all | solution.py:10
  126.7 0.0 copy-done.1
  126.7 0.0 copy-done.2
  126.7 362.4 %all_gather.6 = bf16[2048,16]{0,1:T(8,128)(2,1)S(1)} all-gather(bf16[1024,16]{0,1:T(8,128)(2,1)S(1)} %multiply_convert_fusion), channel_id=1, replica_groups=mesh['trial'=4,'ep'=4,'fsdp'=2] {'fsdp'}, dimensions={0}, use_global_device_ids=true | all-gather | bytes 98304 | tf_op jit(solution)/shard_map/all_gather | solution.py:15
  489.1 5.8 all_gather.7
  494.8 0.0 copy-done
  494.8 0.6 constant_dynamic-slice_fusion
  495.4 0.0 all-to-all-done
  495.5 60.5 %copy.9 = bf16[16,512,2,1024]{3,2,1,0:T(2,128)(2,1)} copy(bf16[16,512,2,1024]{3,0,1,2:T(8,128)(2,1)} %bitcast.1) | data formatting | bytes 67108864 | tf_op jit(solution)/shard_map/all_to_all | solution.py:10
  556.0 54.2 %all_to_all.16 = bf16[16,512,2048]{2,1,0:T(8,128)(2,1)} reshape(bf16[16,512,2,1024]{3,2,1,0:T(2,128)(2,1)} %copy.9) | data formatting | bytes 67108864 | tf_op jit(solution)/shard_map/all_to_all | solution.py:10
  610.2 0.7 copy.15
  (1 shorter events, 0.0 us)
Async XLA Ops:
  7.2 45.3 %all-reduce.2.cloned.1.call-start = ((), (), s32[]{:S(2)}) async-start(), calls=%async_computation.1 | async-start | bytes 131072 | tf_op jit(solution)/shard_map/pmax | solution.py:8
  53.5 73.1 %copy-start.1 = (f32[1024,16]{0,1:T(8,128)S(1)}, f32[1024,16]{0,1:T(8,128)}, u32[]{:S(2)}) copy-start(f32[1024,16]{0,1:T(8,128)} %param.4) | copy-start | bytes 196612
  53.5 73.1 %copy-start.2 = (f32[1024]{0:T(1024)S(1)}, f32[1024]{0:T(1024)}, u32[]{:S(2)}) copy-start(f32[1024]{0:T(1024)} %param.5) | copy-start | bytes 12292
  53.5 441.3 %copy-start = (f32[16,1024]{1,0:T(8,128)S(1)}, f32[16,1024]{1,0:T(8,128)}, u32[]{:S(2)}) copy-start(f32[16,1024]{1,0:T(8,128)} %all-reduce.2.cloned.1.call-done) | copy-start | bytes 196612
  113.7 381.8 %all-to-all-start = ((bf16[16,1024,1024]{2,0,1:T(8,128)(2,1)}), bf16[16,1024,1024]{2,0,1:T(8,128)(2,1)}, u32[]{:S(2)}, u32[]{:S(2)}) async-start(bf16[16,1024,1024]{2,0,1:T(8,128)(2,1)} %fusion), calls=%async_computation | async-start | bytes 67108864 | tf_op jit(solution)/shard_map/all_to_all | solution.py:10
Sparse Core Ops, SparseCore 0:
  28.8 23.6 all-reduce.1
where the time goes:
time: 619 us; the launch traced here: 618 us
  blocking collectives  368 us (59%)
  local copies, waits for them, and re-layouts  117 us (19%)
  other arithmetic  81.6 us (13%)
  waiting for transfers between devices  23.9 us (4%)
  between operations  14.1 us (2%)
  starting transfers between devices  13 us (2%)
    all_gather x1, blocking collectives, shards(): row_router = lax.all_gather(part_router, 'fsdp', axis=0, tiled=True)  362 us
    all_to_all x2, local copies, waits for them, and re-layouts, shards(): lax.all_to_all(narrow_down, 'fsdp', split_axis=1, concat_axis=2, tiled=True)  115 us
    convert_element_type x1, other arithmetic, shards(): (master_down / jnp.expand_dims(scale_down, 2)).astype(jnp.bfloat16)  60.1 us
    pmax x1, waiting for transfers between devices, shards(): scale_down = lax.pmax(jnp.max(jnp.abs(master_down), axis=2), 'fsdp')  23.8 us
    reduce_max x1, other arithmetic, shards(): scale_down = lax.pmax(jnp.max(jnp.abs(master_down), axis=2), 'fsdp')  21.4 us
    all_to_all x1, starting transfers between devices, shards(): lax.all_to_all(narrow_down, 'fsdp', split_axis=1, concat_axis=2, tiled=True)  13 us
  transfers between devices with their start and end apart: 2, of which 1 were waited for; matrix products, arithmetic and copies ran while one was open for 0% of the time, Pallas kernels for 0%

commit v1 on v0

--- a/solution.py
+++ b/solution.py
@@ -7,7 +7,12 @@
 def shards(master_down, router_weight, router_gain):
     scale_down = lax.pmax(jnp.max(jnp.abs(master_down), axis=2), "fsdp")
     narrow_down = (master_down / jnp.expand_dims(scale_down, 2)).astype(jnp.bfloat16)
-    final_down = lax.all_to_all(narrow_down, "fsdp", split_axis=1, concat_axis=2, tiled=True)
+    final_down = jnp.concatenate(
+        lax.all_to_all(
+            jnp.stack(jnp.split(narrow_down, lax.axis_size("fsdp"), axis=1)), "fsdp", 0, 0
+        ),
+        axis=2,
+    )
     scale_down = lax.dynamic_slice_in_dim(
         scale_down, lax.axis_index("fsdp") * final_down.shape[1], final_down.shape[1], axis=1
     )

time: 619 us -> 544 us (0.88)
  local copies, waits for them, and re-layouts: 117 us -> 47.7 us
    all_to_all x2 -> x0, local copies, waits for them, and re-layouts: 115 us -> none  [shards(): lax.all_to_all(narrow_down, 'fsdp', split_axis=1, concat_axis=2, tiled=True)]
    convert_element_type x1, other arithmetic: 60.1 us -> 32.9 us  [shards(): (master_down / jnp.expand_dims(scale_down, 2)).astype(jnp.bfloat16)]
    reshape x0 -> x1, local copies, waits for them, and re-layouts: none -> 23.3 us  [shards(): jnp.concatenate(lax.all_to_all(jnp.stack(jnp.split(narrow_down, lax.axis_...]
    another operation x0 -> x1, local copies, waits for them, and re-layouts: none -> 23.1 us  [shards(): jnp.stack(jnp.split(narrow_down, lax.axis_size('fsdp'), axis=1))]
    another operation x0 -> x1, other arithmetic: none -> 23 us  [shards(): jnp.stack(jnp.split(narrow_down, lax.axis_size('fsdp'), axis=1))]
where the time goes in v1:
time: 544 us
  blocking collectives  368 us (68%)
  other arithmetic  77.3 us (14%)
  local copies, waits for them, and re-layouts  47.7 us (9%)
  waiting for transfers between devices  23.9 us (4%)
  between operations  14.1 us (3%)
  starting transfers between devices  13.1 us (2%)
    all_gather x1, blocking collectives, shards(): row_router = lax.all_gather(part_router, 'fsdp', axis=0, tiled=True)  362 us
    convert_element_type x1, other arithmetic, shards(): (master_down / jnp.expand_dims(scale_down, 2)).astype(jnp.bfloat16)  32.9 us
    pmax x1, waiting for transfers between devices, shards(): scale_down = lax.pmax(jnp.max(jnp.abs(master_down), axis=2), 'fsdp')  23.8 us
    reshape x1, local copies, waits for them, and re-layouts, shards(): jnp.concatenate(lax.all_to_all(jnp.stack(jnp.split(narrow_down, lax.axis_...  23.3 us
    another operation x1, local copies, waits for them, and re-layouts, shards(): jnp.stack(jnp.split(narrow_down, lax.axis_size('fsdp'), axis=1))  23.1 us
    another operation x1, other arithmetic, shards(): jnp.stack(jnp.split(narrow_down, lax.axis_size('fsdp'), axis=1))  23 us
    reduce_max x1, other arithmetic, shards(): scale_down = lax.pmax(jnp.max(jnp.abs(master_down), axis=2), 'fsdp')  21.4 us
    all_to_all x1, starting transfers between devices, shards(): lax.all_to_all(jnp.stack(jnp.split(narrow_down, lax.axis_size('fsdp'), ax...  13.1 us
  transfers between devices with their start and end apart: 2, of which 1 were waited for; matrix products, arithmetic and copies ran while one was open for 0% of the time, Pallas kernels for 0%

profile of v1, /device:TPU:0, one launch (start us, length us, event | category | flops | bytes accessed | tf_op | source)
XLA Modules:
  0.0 544.2 jit_solution(12114528892555993120)
XLA Ops:
  7.2 0.0 all-reduce.2.cloned.1.call-start
  7.2 21.4 %abs_reduce_fusion = f32[16,1024]{1,0:T(8,128)} fusion(f32[16,1024,1024]{2,1,0:T(8,128)} %param.3), kind=kLoop, calls=%fused_computation.1 | loop fusion | flops 33538048 | bytes 67174400 | tf_op jit(solution)/shard_map/reduce_max | solution.py:8
  28.6 0.0 all-reduce.2.cloned.1.call-update
  28.6 23.8 %all-reduce.2.cloned.1.call-done = f32[16,1024]{1,0:T(8,128)} async-done(((f32[16,1024]{1,0:T(8,128)}), f32[16,1024]{1,0:T(8,128)}) %all-reduce.2.cloned.1.call-update) | async-done | bytes 65552 | tf_op jit(solution)/shard_map/pmax | solution.py:8
  52.5 32.9 %divide_convert_fusion = bf16[16,1024,1024]{2,1,0:T(8,128)(2,1)} fusion(f32[16,1024,1024]{2,1,0:T(8,128)} %param.3, f32[16,1024]{1,0:T(8,128)} %all-reduce.2.cloned.1.call-done), kind=kLoop, calls=%fused_computation | loop fusion | flops 33554432 | bytes 100728832 | tf_op jit(solution)/shard_map/convert_element_type | solution.py:9
  85.4 23.1 %slice_bitcast_fusion.1 = (bf16[1,16,512,1024]{3,2,1,0:T(8,128)(2,1)}, bf16[1,16,512,1024]{3,2,1,0:T(8,128)(2,1)}) fusion(bf16[16,1024,1024]{2,1,0:T(8,128)(2,1)} %divide_convert_fusion), kind=kLoop, calls=%fused_computation.4 | loop fusion | bytes 67108864 | tf_op jit(solution)/shard_map/stack | solution.py:12
  108.5 23.0 %pad_maximum_fusion = bf16[2,16,512,1024]{3,2,1,0:T(8,128)(2,1)} fusion(bf16[1,16,512,1024]{3,2,1,0:T(8,128)(2,1)} %get-tuple-element.4, bf16[1,16,512,1024]{3,2,1,0:T(8,128)(2,1)} %get-tuple-element.3), kind=kLoop, calls=%fused_computation.2 | loop fusion | flops 16777216 | bytes 67108864 | tf_op jit(solution)/shard_map/stack | solution.py:12
  131.4 0.0 copy-start.1
  131.4 0.0 copy-start.2
  131.5 0.0 copy-start
  131.5 13.1 %all-to-all-start = ((bf16[2,16,512,1024]{3,2,1,0:T(8,128)(2,1)}), bf16[2,16,512,1024]{3,2,1,0:T(8,128)(2,1)}, u32[]{:S(2)}, u32[]{:S(2)}) async-start(bf16[2,16,512,1024]{3,2,1,0:T(8,128)(2,1)} %pad_maximum_fusion), calls=%async_computation | async-start | bytes 67108864 | tf_op jit(solution)/shard_map/all_to_all | solution.py:11
  144.6 0.0 copy-done.1
  144.6 0.0 copy-done.2
  144.6 362.4 %all_gather.6 = bf16[2048,16]{0,1:T(8,128)(2,1)S(1)} all-gather(bf16[1024,16]{0,1:T(8,128)(2,1)S(1)} %multiply_convert_fusion), channel_id=1, replica_groups=mesh['trial'=4,'ep'=4,'fsdp'=2] {'fsdp'}, dimensions={0}, use_global_device_ids=true | all-gather | bytes 98304 | tf_op jit(solution)/shard_map/all_gather | solution.py:20
  507.0 5.8 %all_gather.7 = bf16[2048,64]{0,1:T(8,128)(2,1)S(1)} all-gather(bf16[2048,16]{0,1:T(8,128)(2,1)S(1)} %all_gather.6), channel_id=1, replica_groups=mesh['trial'=4,'ep'=4,'fsdp'=2] {'ep'}, dimensions={1}, use_global_device_ids=true | all-gather | bytes 327680 | tf_op jit(solution)/shard_map/all_gather | solution.py:21
  512.7 0.0 copy-done
  512.7 0.6 constant_dynamic-slice_fusion
  513.4 0.0 all-to-all-done
  513.4 23.3 %copy.7 = bf16[2,16,64,8,1024]{4,3,0,2,1:T(8,128)(2,1)} copy(bf16[2,16,64,8,1024]{4,3,2,1,0:T(8,128)(2,1)} %bitcast.3) | data formatting | bytes 67108864 | tf_op jit(solution)/shard_map/reshape | solution.py:10
  536.6 0.7 copy.10
  (1 shorter events, 0.0 us)
Async XLA Ops:
  7.2 45.3 %all-reduce.2.cloned.1.call-start = ((), (), s32[]{:S(2)}) async-start(), calls=%async_computation.1 | async-start | bytes 131072 | tf_op jit(solution)/shard_map/pmax | solution.py:8
  131.4 13.2 %copy-start.1 = (f32[1024,16]{0,1:T(8,128)S(1)}, f32[1024,16]{0,1:T(8,128)}, u32[]{:S(2)}) copy-start(f32[1024,16]{0,1:T(8,128)} %param.4) | copy-start | bytes 196612
  131.4 13.2 %copy-start.2 = (f32[1024]{0:T(1024)S(1)}, f32[1024]{0:T(1024)}, u32[]{:S(2)}) copy-start(f32[1024]{0:T(1024)} %param.5) | copy-start | bytes 12292
  131.5 381.3 %copy-start = (f32[16,1024]{1,0:T(8,128)S(1)}, f32[16,1024]{1,0:T(8,128)}, u32[]{:S(2)}) copy-start(f32[16,1024]{1,0:T(8,128)} %all-reduce.2.cloned.1.call-done) | copy-start | bytes 196612
  131.5 381.9 %all-to-all-start = ((bf16[2,16,512,1024]{3,2,1,0:T(8,128)(2,1)}), bf16[2,16,512,1024]{3,2,1,0:T(8,128)(2,1)}, u32[]{:S(2)}, u32[]{:S(2)}) async-start(bf16[2,16,512,1024]{3,2,1,0:T(8,128)(2,1)} %pad_maximum_fusion), calls=%async_computation | async-start | bytes 67108864 | tf_op jit(solution)/shard_map/all_to_all | solution.py:11
Sparse Core Ops, SparseCore 0:
  28.8 23.6 all-reduce.1
